TPU v7x, 32 devices: a whole 2x2x4 slice. The times are simulated.
32 devices in a mesh: path: 16 (over z, x, core), shard: 2 (over y).
Axes of the slice: x: 2, y: 2, z: 4, core: 2. Of those that a mesh axis runs over, the one named last changes fastest.
Arguments:
- deltas: bfloat16 [16, 32, 4096], P('path', 'shard'), may hold values from -96 to 96
- momentum: float32 [16, 32, 4096], P(None, 'shard', 'path'), may hold values from -4 to 4
- path_module: int32 [16], replicated, may hold values from 0 to 15, as said below
Outputs:
- path_update: bfloat16 [16, 32, 4096], P('path', 'shard')
- new_momentum: float32 [16, 32, 4096], P(None, 'shard', 'path')
Inputs may be any that keep to these rules, and one draw needn't show every extreme that they name: `path_module`: every module is used by at least one and at most seven paths.
All inputs are finite; a program needn't handle non-finite values.
Results may differ from a plain program's by a relative error of at most 0.0004.
Values may be sent and summed in bfloat16 or wider, within the bound.
A program may use at most 64 MiB of HBM per device.

v0:
```python
import jax
import jax.numpy as jnp
from jax import lax
from jax.sharding import PartitionSpec as P

D = 4096
outer_rate = 0.7
momentum_rate = 0.9
clip_ratio = 2.0


def local(deltas, momentum, path_module):
    own_index = lax.axis_index("path")
    modules = momentum.shape[0]
    row_count = deltas.shape[1]
    onehot = (path_module[:, None] == jnp.arange(modules, dtype=jnp.int32)[None, :]).astype(
        jnp.float32
    )
    counts = jnp.sum(onehot, axis=0)
    own_module = lax.dynamic_index_in_dim(path_module, own_index, 0, keepdims=False)
    column_pieces = lax.all_to_all(deltas, "path", split_axis=2, concat_axis=0, tiled=True)
    totals = jnp.einsum(
        "pm,prc->mrc",
        onehot.astype(jnp.bfloat16),
        column_pieces,
        preferred_element_type=jnp.float32,
    )
    outer_grad = totals / counts[:, None, None]
    local_squares = jnp.sum(outer_grad * outer_grad, axis=(1, 2))
    norm_squares = lax.psum(local_squares, ("path", "shard"))
    limit = clip_ratio * jnp.sqrt(jnp.float32(row_count * lax.axis_size("shard") * D))
    shrink = jnp.minimum(1.0, limit / jnp.sqrt(norm_squares + 1e-06))
    clipped = outer_grad * shrink[:, None, None]
    new_momentum = momentum_rate * momentum + clipped
    outer_step = (outer_rate * (clipped + momentum_rate * new_momentum)).astype(jnp.bfloat16)
    gathered = lax.all_gather(outer_step, "path", axis=2, tiled=True)
    path_update = lax.dynamic_index_in_dim(gathered, own_module, 0, keepdims=True)
    return (path_update, new_momentum)


def solution(mesh):
    return jax.shard_map(
        local,
        mesh=mesh,
        in_specs=(P("path", "shard", None), P(None, "shard", "path"), P()),
        out_specs=(P("path", "shard", None), P(None, "shard", "path")),
        check_vma=False,
    )
```

profile of v0, /device:TPU:0, one launch (start us, length us, event | category | flops | bytes accessed | tf_op | source)
XLA Modules:
  0.0 145.2 jit_solution(7055501070345371449)
XLA Ops:
  7.2 4.3 %copy.8 = bf16[1,16,4096]{1,0,2:T(2,128)(2,1)S(1)} copy(bf16[1,16,4096]{2,1,0:T(8,128)(2,1)} %param.3) | data formatting | bytes 262144 | tf_op args[0]
  11.5 0.5 broadcast.26
  12.0 0.0 copy-start.1
  12.0 22.4 %reduce = bf16[4096,16]{1,0:T(8,128)(2,1)S(1)} reduce(bf16[4096,1,16]{2,1,0:T(2,128)(2,1)S(1)} %bitcast.25, bf16[]{:T(256)} %broadcast.26), dimensions={1}, to_apply=%bitcast.15.reduce_sub_computation | reduce | bytes 262146
  34.4 1.8 %reshape.8 = bf16[16,2,2048]{2,1,0:T(2,128)(2,1)} reshape(bf16[4096,16]{1,0:T(8,128)(2,1)S(1)} %reduce) | data formatting | bytes 262144
  36.2 7.4 %all-to-all-start = ((bf16[16,2,2048]{2,1,0:T(2,128)(2,1)}), bf16[16,2,2048]{2,1,0:T(2,128)(2,1)S(1)}, u32[]{:S(2)}, u32[]{:S(2)}) async-start(bf16[16,2,2048]{2,1,0:T(2,128)(2,1)} %reshape.8), calls=%async_computation | async-start | bytes 262144 | tf_op jit(solution)/shard_map/all_to_all | solution.py:21
  43.6 0.0 all-gather.2.cloned.1.call-start
  43.6 0.0 copy-done.1
  43.6 0.1 convert_reduce_fusion
  43.8 7.7 %all-to-all-done = bf16[16,2,2048]{2,1,0:T(2,128)(2,1)S(1)} async-done(((bf16[16,2,2048]{2,1,0:T(2,128)(2,1)}), bf16[16,2,2048]{2,1,0:T(2,128)(2,1)S(1)}, u32[]{:S(2)}, u32[]{:S(2)}) %all-to-all-start) | async-done | bytes 131104 | tf_op jit(solution)/shard_map/all_to_all | solution.py:21
  51.5 1.8 %reshape.9 = bf16[4096,1,16]{2,1,0:T(2,128)(2,1)S(1)} reshape(bf16[16,2,2048]{2,1,0:T(2,128)(2,1)S(1)} %all-to-all-done) | data formatting | bytes 262144
  53.3 0.0 copy-start
  53.3 2.0 %copy.9 = bf16[1,16,4096]{2,1,0:T(8,128)(2,1)S(1)} copy(bf16[1,16,4096]{1,0,2:T(2,128)(2,1)S(1)} %bitcast.26) | data formatting | bytes 262144 | tf_op jit(solution)/shard_map/all_to_all | solution.py:21
  55.3 0.3 multiply_reduce_fusion
  55.6 37.5 %psum.7 = f32[16]{0:T(128)S(1)} all-reduce(f32[16]{0:T(128)S(1)} %get-tuple-element.8), channel_id=1, replica_groups=mesh['path'=16,'shard'=2] {'path','shard'}, use_global_device_ids=true, to_apply=%region_2.3 | all-reduce | flops 16 | bytes 128 | tf_op jit(solution)/shard_map/psum | solution.py:30
  93.1 0.0 copy-done
  93.1 0.9 fusion
  94.0 0.0 all-gather.2.cloned.1.call-update
  94.0 0.6 dynamic_slice.8
  96.5 0.9 copy.12
  97.4 38.6 %all-gather.2.cloned.1.call-done = bf16[16,16,4096]{2,0,1:T(8,128)(2,1)} async-done(((bf16[16,16,256]{2,0,1:T(8,128)(2,1)}), bf16[16,16,4096]{2,0,1:T(8,128)(2,1)}) %all-gather.2.cloned.1.call-update) | async-done | bytes 2097168 | tf_op jit(solution)/shard_map/all_gather | solution.py:36
  136.0 1.5 %constant_dynamic-slice_fusion = bf16[1,16,4096]{2,0,1:T(2,128)(2,1)S(1)} fusion(bf16[16,16,4096]{2,0,1:T(8,128)(2,1)} %all-gather.2.cloned.1.call-done, s32[]{:T(128)S(6)} %select_n.9), kind=kLoop, calls=%fused_computation.12 | loop fusion | bytes 262148 | tf_op jit(solution)/shard_map/jit(dynamic_index_in_dim)/dynamic_slice | solution.py:37
  137.5 0.8 copy.11
  (2 shorter events, 0.0 us)
Async XLA Ops:
  12.0 31.6 %copy-start.1 = (s32[16]{0:T(128)S(1)}, s32[16]{0:T(128)}, u32[]{:S(2)}) copy-start(s32[16]{0:T(128)} %param.5) | copy-start | bytes 196
  36.2 15.3 %all-to-all-start = ((bf16[16,2,2048]{2,1,0:T(2,128)(2,1)}), bf16[16,2,2048]{2,1,0:T(2,128)(2,1)S(1)}, u32[]{:S(2)}, u32[]{:S(2)}) async-start(bf16[16,2,2048]{2,1,0:T(2,128)(2,1)} %reshape.8), calls=%async_computation | async-start | bytes 262144 | tf_op jit(solution)/shard_map/all_to_all | solution.py:21
  43.6 92.4 %all-gather.2.cloned.1.call-start = ((), (), s32[]{:S(2)}) async-start(), calls=%async_computation.1 | async-start | bytes 2228224 | tf_op jit(solution)/shard_map/all_gather | solution.py:36
  53.3 39.8 %copy-start = (f32[16,16,256]{2,1,0:T(8,128)S(1)}, f32[16,16,256]{2,1,0:T(8,128)}, u32[]{:S(2)}) copy-start(f32[16,16,256]{2,1,0:T(8,128)} %param.4) | copy-start | bytes 786436
Sparse Core Ops, SparseCore 0:
  94.1 41.7 all-gather.1
where the time goes:
time: 146 us; the launch traced here: 145 us
  waiting for transfers between devices  46.3 us (32%)
  blocking collectives  37.5 us (26%)
  other arithmetic  23.4 us (16%)
  between operations  16 us (11%)
  local copies, waits for them, and re-layouts  14.2 us (10%)
  starting transfers between devices  7.43 us (5%)
    all_gather x1, waiting for transfers between devices, local(): gathered = lax.all_gather(outer_step, 'path', axis=2, tiled=True)  38.6 us
    psum x1, blocking collectives, local(): norm_squares = lax.psum(local_squares, ('path', 'shard'))  37.5 us
    unnamed x1, other arithmetic  22.4 us
    unnamed x11, local copies, waits for them, and re-layouts  10.1 us
    all_to_all x1, waiting for transfers between devices, local(): lax.all_to_all(deltas, 'path', split_axis=2, concat_axis=0, tiled=True)  7.73 us
    all_to_all x1, starting transfers between devices, local(): lax.all_to_all(deltas, 'path', split_axis=2, concat_axis=0, tiled=True)  7.39 us
  transfers between devices with their start and end apart: 2, of which 2 were waited for; matrix products, arithmetic and copies ran while one was open for 1% of the time, Pallas kernels for 0%

commit v1 on v0

--- a/solution.py
+++ b/solution.py
@@ -18,7 +18,10 @@
     )
     counts = jnp.sum(onehot, axis=0)
     own_module = lax.dynamic_index_in_dim(path_module, own_index, 0, keepdims=False)
-    column_pieces = lax.all_to_all(deltas, "path", split_axis=2, concat_axis=0, tiled=True)
+    column_pieces = jnp.concatenate(
+        lax.all_to_all(jnp.stack(jnp.split(deltas, lax.axis_size("path"), axis=2)), "path", 0, 0),
+        axis=0,
+    )
     totals = jnp.einsum(
         "pm,prc->mrc",
         onehot.astype(jnp.bfloat16),

time: 146 us -> 136 us (0.932)
  other arithmetic: 23.4 us -> 2.59 us
  local copies, waits for them, and re-layouts: 14.2 us -> 24.5 us
    unnamed x1 -> x0, other arithmetic: 22.4 us -> none
    unnamed x11 -> x19, local copies, waits for them, and re-layouts: 10.1 us -> 21.1 us
    all_to_all x1 -> x0, local copies, waits for them, and re-layouts: 1.99 us -> none  [local(): lax.all_to_all(deltas, 'path', split_axis=2, concat_axis=0, tiled=True)]
  transfers between devices with their start and end apart: 2 -> 2, of which waited for: 2 -> 2; matrix products, arithmetic and copies ran while one was open for 1% -> 2% of each run, Pallas kernels for 0% -> 0%
where the time goes in v1:
time: 136 us; the launch traced here: 135 us
  waiting for transfers between devices  45.7 us (34%)
  blocking collectives  37.5 us (28%)
  local copies, waits for them, and re-layouts  24.5 us (18%)
  between operations  16 us (12%)
  starting transfers between devices  7.43 us (5%)
  other arithmetic  2.59 us (2%)
    all_gather x1, waiting for transfers between devices, local(): gathered = lax.all_gather(outer_step, 'path', axis=2, tiled=True)  38.6 us
    psum x1, blocking collectives, local(): norm_squares = lax.psum(local_squares, ('path', 'shard'))  37.5 us
    unnamed x19, local copies, waits for them, and re-layouts  21.1 us
    all_to_all x1, starting transfers between devices, local(): lax.all_to_all(jnp.stack(jnp.split(deltas, lax.axis_size('path'), axis=2)...  7.39 us
    all_to_all x1, waiting for transfers between devices, local(): lax.all_to_all(jnp.stack(jnp.split(deltas, lax.axis_size('path'), axis=2)...  7.08 us
  transfers between devices with their start and end apart: 2, of which 2 were waited for; matrix products, arithmetic and copies ran while one was open for 2% of the time, Pallas kernels for 0%

profile of v1, /device:TPU:0, one launch (start us, length us, event | category | flops | bytes accessed | tf_op | source)
XLA Modules:
  0.0 134.6 jit_solution(11604103474847722523)
XLA Ops:
  7.2 0.0 copy-start
  7.2 1.3 constant_dynamic-update-slice_fusion.15
  8.5 1.3 constant_dynamic-update-slice_fusion.14
  9.8 1.3 constant_dynamic-update-slice_fusion.13
  11.1 1.3 constant_dynamic-update-slice_fusion.12
  12.4 1.3 constant_dynamic-update-slice_fusion.11
  13.7 1.3 constant_dynamic-update-slice_fusion.10
  15.0 1.3 constant_dynamic-update-slice_fusion.9
  16.2 1.3 constant_dynamic-update-slice_fusion.8
  17.5 1.3 constant_dynamic-update-slice_fusion.7
  18.8 1.3 constant_dynamic-update-slice_fusion.6
  20.1 1.3 constant_dynamic-update-slice_fusion.5
  21.4 1.3 constant_dynamic-update-slice_fusion.4
  22.7 1.3 constant_dynamic-update-slice_fusion.3
  24.0 1.3 constant_dynamic-update-slice_fusion.2
  25.3 1.3 constant_dynamic-update-slice_fusion.1
  26.6 1.3 constant_dynamic-update-slice_fusion
  27.9 7.4 %all-to-all-start = ((bf16[16,1,16,256]{3,2,1,0:T(8,128)(2,1)}), bf16[16,1,16,256]{3,2,1,0:T(8,128)(2,1)S(1)}, u32[]{:S(2)}, u32[]{:S(2)}) async-start(bf16[16,1,16,256]{3,2,1,0:T(8,128)(2,1)} %constant_dynamic-update-slice_fusion), calls=%async_computation | async-start | bytes 262144 | tf_op jit(solution)/shard_map/all_to_all | solution.py:22
  35.3 0.0 all-gather.2.cloned.1.call-start
  35.3 0.8 convert_reduce_fusion
  36.1 7.1 %all-to-all-done = bf16[16,1,16,256]{3,2,1,0:T(8,128)(2,1)S(1)} async-done(((bf16[16,1,16,256]{3,2,1,0:T(8,128)(2,1)}), bf16[16,1,16,256]{3,2,1,0:T(8,128)(2,1)S(1)}, u32[]{:S(2)}, u32[]{:S(2)}) %all-to-all-start) | async-done | bytes 131104 | tf_op jit(solution)/shard_map/all_to_all | solution.py:22
  43.2 0.9 multiply_reduce_fusion
  44.1 37.5 %psum.7 = f32[16]{0:T(128)S(1)} all-reduce(f32[16]{0:T(128)S(1)} %get-tuple-element.10), channel_id=1, replica_groups=mesh['path'=16,'shard'=2] {'path','shard'}, use_global_device_ids=true, to_apply=%region_2.3 | all-reduce | flops 16 | bytes 128 | tf_op jit(solution)/shard_map/psum | solution.py:33
  81.6 1.8 %fusion = (f32[16,16,256]{2,0,1:T(8,128)S(1)}, bf16[16,16,256]{2,0,1:T(8,128)(2,1)}) fusion(f32[16,16,256]{2,1,0:T(8,128)} %param.4, f32[16,16,256]{2,0,1:T(8,128)S(1)} %get-tuple-element.11, f32[16]{0:T(128)S(1)} %multiply_minimum_fusion), kind=kLoop, calls=%fused_computation.2 | loop fusion | flops 458752 | bytes 917568 | tf_op jit(solution)/shard_map/add | solution.py:37
  83.4 0.0 all-gather.2.cloned.1.call-update
  83.5 0.0 copy-done
  83.5 0.6 dynamic_slice.8
  86.0 0.9 copy.30
  86.9 38.6 %all-gather.2.cloned.1.call-done = bf16[16,16,4096]{2,0,1:T(8,128)(2,1)} async-done(((bf16[16,16,256]{2,0,1:T(8,128)(2,1)}), bf16[16,16,4096]{2,0,1:T(8,128)(2,1)}) %all-gather.2.cloned.1.call-update) | async-done | bytes 2097168 | tf_op jit(solution)/shard_map/all_gather | solution.py:39
  125.4 1.5 %constant_dynamic-slice_fusion = bf16[1,16,4096]{2,0,1:T(2,128)(2,1)S(1)} fusion(bf16[16,16,4096]{2,0,1:T(8,128)(2,1)} %all-gather.2.cloned.1.call-done, s32[]{:T(128)S(6)} %select_n.9), kind=kLoop, calls=%fused_computation.29 | loop fusion | bytes 262148 | tf_op jit(solution)/shard_map/jit(dynamic_index_in_dim)/dynamic_slice | solution.py:40
  127.0 0.8 copy.29
  (1 shorter events, 0.0 us)
Async XLA Ops:
  7.2 76.3 %copy-start = (s32[16]{0:T(128)S(1)}, s32[16]{0:T(128)}, u32[]{:S(2)}) copy-start(s32[16]{0:T(128)} %param.5) | copy-start | bytes 196
  27.9 15.3 %all-to-all-start = ((bf16[16,1,16,256]{3,2,1,0:T(8,128)(2,1)}), bf16[16,1,16,256]{3,2,1,0:T(8,128)(2,1)S(1)}, u32[]{:S(2)}, u32[]{:S(2)}) async-start(bf16[16,1,16,256]{3,2,1,0:T(8,128)(2,1)} %constant_dynamic-update-slice_fusion), calls=%async_computation | async-start | bytes 262144 | tf_op jit(solution)/shard_map/all_to_all | solution.py:22
  35.3 90.1 %all-gather.2.cloned.1.call-start = ((), (), s32[]{:S(2)}) async-start(), calls=%async_computation.1 | async-start | bytes 2228224 | tf_op jit(solution)/shard_map/all_gather | solution.py:39
Sparse Core Ops, SparseCore 0:
  83.6 41.7 all-gather.1
